TPU v7x, 32 devices: a whole 2x2x4 slice. The times are simulated.
32 devices in a mesh: dp: 4 (over z), tp: 8 (over y, x, core).
Axes of the slice: x: 2, y: 2, z: 4, core: 2. Of those that a mesh axis runs over, the one named last changes fastest.
Arguments:
- layer_input: bfloat16 [8192, 2048], P(('dp', 'tp')), may hold values from -6 to 6
- segments: int32 [4, 2048], P('dp'), may hold values from 0 to 1, as said below
- norm_gains: float32 [2, 2048], replicated, may hold values from 0.25 to 1.75
- norm_biases: float32 [2, 2048], replicated, may hold values from -2 to 2
- w_qkv: bfloat16 [2048, 3, 2048], P(None, None, 'tp'), may hold values from -0.125 to 0.125
- qv_bias: float32 [2, 2048], P(None, 'tp'), may hold values from -2 to 2
- key_bias: float32 [32, 16], P('tp'), may hold values from -3 to 3
- w_out: bfloat16 [2048, 2048], P('tp'), may hold values from -2 to 2
- w_gate_up: bfloat16 [2048, 2, 5632], P(None, None, 'tp'), may hold values from -0.125 to 0.125
- w_down: bfloat16 [5632, 2048], P('tp'), may hold values from -0.078125 to 0.078125
- out_grad: bfloat16 [8192, 2048], P(('dp', 'tp')), may hold values from -6 to 6
Outputs:
- output: float32 [8192, 2048], P(('dp', 'tp'))
- grad_x: float32 [8192, 2048], P(('dp', 'tp'))
- grad_qkv: float32 [2048, 3, 2048], P(None, None, 'tp')
- grad_qv_bias: float32 [2, 2048], P(None, 'tp')
- grad_key_bias: float32 [32, 16], P('tp')
- grad_out: float32 [2048, 2048], P('tp')
- grad_gate_up: float32 [2048, 2, 5632], P(None, None, 'tp')
- grad_down: float32 [5632, 2048], P('tp')
- grad_gains: float32 [2, 2048], P(None, 'tp')
- grad_biases: float32 [2, 2048], P(None, 'tp')
Inputs may be any that keep to these rules, and one draw needn't show every extreme that they name: `segments`: in each group the ids number the documents from 0 and never fall; every document has 1024 tokens or more.
All inputs are finite; a program needn't handle non-finite values.
Results may differ from a plain program's by a relative error of at most 0.023.
Values may be sent and summed in bfloat16 or wider, within the bound.
A program may use at most 256 MiB of HBM per device.

v0:
```python
import math
import jax
import jax.numpy as jnp
from jax import lax
from jax.sharding import PartitionSpec as P

D = 2048
HEAD_DIM = 64
ROT = 16
EPSILON = 1e-05


def norm_forward(values, gain, shift_bias):
    centre = jnp.mean(values, axis=-1, keepdims=True)
    centred = values - centre
    spread = jnp.mean(centred * centred, axis=-1, keepdims=True)
    inverse = lax.rsqrt(spread + EPSILON)
    normed = centred * inverse
    return (normed * gain + shift_bias, normed, inverse)


def norm_backward(grad_normed, normed, inverse, gain):
    scaled = grad_normed * gain
    inner = jnp.mean(scaled, axis=-1, keepdims=True)
    along = jnp.mean(scaled * normed, axis=-1, keepdims=True)
    return (
        inverse * (scaled - inner - normed * along),
        jnp.sum(grad_normed * normed, axis=0),
        jnp.sum(grad_normed, axis=0),
    )


def rotary_tables(segment_ids):
    places = jnp.arange(segment_ids.shape[0], dtype=jnp.int32)
    starts_here = jnp.concatenate(
        [jnp.ones((1,), dtype=jnp.bool_), segment_ids[1:] != segment_ids[:-1]]
    )
    doc_start = lax.cummax(jnp.where(starts_here, places, 0), axis=0)
    positions = (places - doc_start).astype(jnp.float32)
    halves = ROT // 2
    frequency = jnp.exp(jnp.arange(halves, dtype=jnp.float32) * (-2.0 * math.log(10000.0) / ROT))
    angles = positions[:, None] * frequency[None, :]
    return (jnp.cos(angles)[:, None, :], jnp.sin(angles)[:, None, :])


def rotate(tensor, cosine, sine):
    halves = ROT // 2
    first_half = tensor[..., :halves]
    second_half = tensor[..., halves:ROT]
    return jnp.concatenate(
        [
            first_half * cosine - second_half * sine,
            second_half * cosine + first_half * sine,
            tensor[..., ROT:],
        ],
        axis=-1,
    )


def rotate_back(tensor, cosine, sine):
    halves = ROT // 2
    first_half = tensor[..., :halves]
    second_half = tensor[..., halves:ROT]
    return jnp.concatenate(
        [
            first_half * cosine + second_half * sine,
            second_half * cosine - first_half * sine,
            tensor[..., ROT:],
        ],
        axis=-1,
    )


def contract_rows(left, right):
    return lax.dot_general(
        left, right, (((0,), (0,)), ((), ())), preferred_element_type=jnp.float32
    )


def contract_cols(left, right):
    return lax.dot_general(
        left, right, (((1,), (1,)), ((), ())), preferred_element_type=jnp.float32
    )


def local(
    layer_input,
    segments,
    norm_gains,
    norm_biases,
    w_qkv,
    qv_bias,
    key_bias,
    w_out,
    w_gate_up,
    w_down,
    out_grad,
):
    segment_ids = segments[0]
    group_rows = segment_ids.shape[0]
    local_width = w_qkv.shape[2]
    local_heads = local_width // HEAD_DIM
    local_hidden = w_down.shape[0]
    block_rows = min(512, group_rows)
    blocks = group_rows // block_rows
    scale = HEAD_DIM ** (-0.5)
    places = jnp.arange(group_rows, dtype=jnp.int32)
    cosine, sine = rotary_tables(segment_ids)
    qkv_matrix = w_qkv.reshape(D, 3 * local_width)
    gate_matrix = w_gate_up.reshape(D, 2 * local_hidden)
    x_float = layer_input.astype(jnp.float32)
    normed_one, hat_one, inverse_one = norm_forward(x_float, norm_gains[0], norm_biases[0])
    rows_one = lax.all_gather(normed_one.astype(jnp.bfloat16), "tp", axis=0, tiled=True)
    projected = jnp.dot(rows_one, qkv_matrix, preferred_element_type=jnp.float32).reshape(
        group_rows, 3, local_heads, HEAD_DIM
    )
    key_full = jnp.concatenate(
        [key_bias, jnp.zeros((local_heads, HEAD_DIM - ROT), jnp.float32)], axis=1
    )
    bias_all = jnp.stack(
        [
            qv_bias[0].reshape(local_heads, HEAD_DIM),
            key_full,
            qv_bias[1].reshape(local_heads, HEAD_DIM),
        ]
    )
    projected = projected + bias_all[None]
    queries = rotate(projected[:, 0], cosine, sine).astype(jnp.bfloat16)
    key_rows = rotate(projected[:, 1], cosine, sine).astype(jnp.bfloat16)
    value_rows = projected[:, 2].astype(jnp.bfloat16)
    query_blocks = queries.reshape(blocks, block_rows, local_heads, HEAD_DIM)
    segment_blocks = segment_ids.reshape(blocks, block_rows)
    place_blocks = places.reshape(blocks, block_rows)

    def scores_of(query_block, segment_block, place_block):
        raw = (
            jnp.einsum("bhd,khd->hbk", query_block, key_rows, preferred_element_type=jnp.float32)
            * scale
        )
        visible = (segment_block[:, None] == segment_ids[None, :]) & (
            place_block[:, None] >= places[None, :]
        )
        return jnp.where(visible[None], raw, -jnp.inf)

    def forward_block(item):
        query_block, segment_block, place_block = item
        scores = scores_of(query_block, segment_block, place_block)
        highest = jnp.max(scores, axis=-1, keepdims=True)
        expo = jnp.exp(scores - highest)
        totals = jnp.sum(expo, axis=-1, keepdims=True)
        probs = (expo / totals).astype(jnp.bfloat16)
        mixed = jnp.einsum("hbk,khd->bhd", probs, value_rows, preferred_element_type=jnp.float32)
        return (mixed.astype(jnp.bfloat16), (highest + jnp.log(totals))[..., 0])

    attended, log_totals = lax.map(forward_block, (query_blocks, segment_blocks, place_blocks))
    attended = attended.reshape(group_rows, local_width)
    hidden_state = x_float + lax.psum_scatter(
        jnp.dot(attended, w_out, preferred_element_type=jnp.float32).astype(jnp.bfloat16),
        "tp",
        scatter_dimension=0,
        tiled=True,
    ).astype(jnp.float32)
    normed_two, hat_two, inverse_two = norm_forward(hidden_state, norm_gains[1], norm_biases[1])
    rows_two = lax.all_gather(normed_two.astype(jnp.bfloat16), "tp", axis=0, tiled=True)
    gate_up = jnp.dot(rows_two, gate_matrix, preferred_element_type=jnp.float32).reshape(
        group_rows, 2, local_hidden
    )
    gate_part = gate_up[:, 0]
    up_part = gate_up[:, 1]
    sigmoid_gate = jax.nn.sigmoid(gate_part)
    silu_gate = gate_part * sigmoid_gate
    activation = (silu_gate * up_part).astype(jnp.bfloat16)
    output = hidden_state + lax.psum_scatter(
        jnp.dot(activation, w_down, preferred_element_type=jnp.float32).astype(jnp.bfloat16),
        "tp",
        scatter_dimension=0,
        tiled=True,
    ).astype(jnp.float32)
    grad_float = out_grad.astype(jnp.float32)
    portion = lax.all_gather(out_grad, "tp", axis=0, tiled=True)
    weight_sum = contract_rows(activation, portion)
    grad_act = contract_cols(portion, w_down)
    grad_down, grad_act = (weight_sum, grad_act)
    grad_gate = grad_act * up_part * sigmoid_gate * (1.0 + gate_part * (1.0 - sigmoid_gate))
    grad_up = grad_act * silu_gate
    grad_pair = (
        jnp.stack([grad_gate, grad_up], axis=1)
        .astype(jnp.bfloat16)
        .reshape(group_rows, 2 * local_hidden)
    )
    grad_gate_up = contract_rows(rows_two, grad_pair).reshape(D, 2, local_hidden)
    grad_normed_two = lax.psum_scatter(
        contract_cols(grad_pair, gate_matrix).astype(jnp.bfloat16),
        "tp",
        scatter_dimension=0,
        tiled=True,
    ).astype(jnp.float32)
    back_two, gain_two, shift_two = norm_backward(
        grad_normed_two, hat_two, inverse_two, norm_gains[1]
    )
    grad_hidden = grad_float + back_two
    portion = lax.all_gather(grad_hidden.astype(jnp.bfloat16), "tp", axis=0, tiled=True)
    weight_sum = contract_rows(attended, portion)
    grad_att = contract_cols(portion, w_out)
    grad_out = weight_sum
    grad_blocks = grad_att.astype(jnp.bfloat16).reshape(blocks, block_rows, local_heads, HEAD_DIM)

    def backward_block(running, item):
        grad_keys, grad_values = running
        query_block, grad_block, log_block, segment_block, place_block = item
        scores = scores_of(query_block, segment_block, place_block)
        weights = jnp.exp(scores - log_block[..., None])
        grad_values = grad_values + jnp.einsum(
            "hbk,bhd->khd",
            weights.astype(jnp.bfloat16),
            grad_block,
            preferred_element_type=jnp.float32,
        )
        grad_weights = jnp.einsum(
            "bhd,khd->hbk", grad_block, value_rows, preferred_element_type=jnp.float32
        )
        inner = jnp.sum(weights * grad_weights, axis=-1, keepdims=True)
        grad_scores = (weights * (grad_weights - inner)).astype(jnp.bfloat16)
        grad_query = (
            jnp.einsum("hbk,khd->bhd", grad_scores, key_rows, preferred_element_type=jnp.float32)
            * scale
        )
        grad_keys = (
            grad_keys
            + jnp.einsum(
                "hbk,bhd->khd", grad_scores, query_block, preferred_element_type=jnp.float32
            )
            * scale
        )
        return ((grad_keys, grad_values), grad_query)

    zero_heads = jnp.zeros((group_rows, local_heads, HEAD_DIM), jnp.float32)
    (grad_keys, grad_values), grad_queries = lax.scan(
        backward_block,
        (zero_heads, zero_heads),
        (query_blocks, grad_blocks, log_totals, segment_blocks, place_blocks),
    )
    grad_queries = grad_queries.reshape(group_rows, local_heads, HEAD_DIM)
    grad_projected = jnp.stack(
        [
            rotate_back(grad_queries, cosine, sine),
            rotate_back(grad_keys, cosine, sine),
            grad_values,
        ],
        axis=1,
    ).astype(jnp.bfloat16)
    bias_sums = jnp.sum(grad_projected, axis=0, dtype=jnp.float32)
    grad_qv = jnp.stack([bias_sums[0].reshape(local_width), bias_sums[2].reshape(local_width)])
    grad_key = bias_sums[1][:, :ROT]
    grad_flat = grad_projected.reshape(group_rows, 3 * local_width)
    grad_qkv = contract_rows(rows_one, grad_flat).reshape(D, 3, local_width)
    grad_normed_one = lax.psum_scatter(
        contract_cols(grad_flat, qkv_matrix).astype(jnp.bfloat16),
        "tp",
        scatter_dimension=0,
        tiled=True,
    ).astype(jnp.float32)
    back_one, gain_one, shift_one = norm_backward(
        grad_normed_one, hat_one, inverse_one, norm_gains[0]
    )
    grad_input = grad_hidden + back_one
    gain_grads, shift_grads = (
        lax.psum_scatter(
            jnp.stack([gain_one, gain_two]).astype(jnp.bfloat16),
            "tp",
            scatter_dimension=1,
            tiled=True,
        ).astype(jnp.float32),
        lax.psum_scatter(
            jnp.stack([shift_one, shift_two]).astype(jnp.bfloat16),
            "tp",
            scatter_dimension=1,
            tiled=True,
        ).astype(jnp.float32),
    )
    grad_qkv, grad_qv, grad_key, grad_out, grad_gate_up, grad_down, gain_grads, shift_grads = (
        lax.psum(grad_qkv.astype(jnp.bfloat16), "dp").astype(jnp.float32),
        lax.psum(grad_qv.astype(jnp.bfloat16), "dp").astype(jnp.float32),
        lax.psum(grad_key.astype(jnp.bfloat16), "dp").astype(jnp.float32),
        lax.psum(grad_out.astype(jnp.bfloat16), "dp").astype(jnp.float32),
        lax.psum(grad_gate_up.astype(jnp.bfloat16), "dp").astype(jnp.float32),
        lax.psum(grad_down.astype(jnp.bfloat16), "dp").astype(jnp.float32),
        lax.psum(gain_grads.astype(jnp.bfloat16), "dp").astype(jnp.float32),
        lax.psum(shift_grads.astype(jnp.bfloat16), "dp").astype(jnp.float32),
    )
    return (
        output,
        grad_input,
        grad_qkv,
        grad_qv,
        grad_key,
        grad_out,
        grad_gate_up,
        grad_down,
        gain_grads,
        shift_grads,
    )


def solution(mesh):
    in_specs = (
        P(("dp", "tp"), None),
        P("dp", None),
        P(),
        P(),
        P(None, None, "tp"),
        P(None, "tp"),
        P("tp", None),
        P("tp", None),
        P(None, None, "tp"),
        P("tp", None),
        P(("dp", "tp"), None),
    )
    out_specs = (
        P(("dp", "tp"), None),
        P(("dp", "tp"), None),
        P(None, None, "tp"),
        P(None, "tp"),
        P("tp", None),
        P("tp", None),
        P(None, None, "tp"),
        P("tp", None),
        P(None, "tp"),
        P(None, "tp"),
    )
    return jax.shard_map(local, mesh=mesh, in_specs=in_specs, out_specs=out_specs, check_vma=False)
```

profile of v0, /device:TPU:0, one launch (start us, length us, event | category | flops | bytes accessed | tf_op | source)
XLA Modules:
  0.0 1480.7 jit_solution(10848038059797148822)
XLA Ops:
  23.3 49.9 %all-gather.5.cloned.1.call-done = bf16[2048,2048]{1,0:T(8,128)(2,1)} async-done(((bf16[256,2048]{1,0:T(8,128)(2,1)}), bf16[2048,2048]{1,0:T(8,128)(2,1)}) %all-gather.5.cloned.1.call-update) | async-done | bytes 8388624 | tf_op jit(solution)/shard_map/all_gather | solution.py:113
  73.2 10.1 fusion.63
  88.5 63.9 %while.28 = (s32[]{:T(128)}, bf16[4,512,4,64]{1,3,2,0:T(8,128)(2,1)}, f32[4,4,512]{2,1,0:T(4,128)S(1)}, s32[4,512]{1,0:T(4,128)S(1)}, s32[1,2048]{1,0:T(1,128)S(...) while((s32[]{:T(128)}, ...), condition=%wide.region_7.8_spmd.clone, body=%wide.region_4.7_spmd.clone.sunk | while | flops 1127348224 | bytes 61427864 | solution.py:155
  98.5 5.9 fusion.150
  114.4 5.9 fusion.150
  130.3 5.9 fusion.150
  146.3 5.9 fusion.150
  155.8 5.8 convolution_convert_fusion.2
  161.7 71.6 %reduce-scatter.11.cloned.1.call-done = bf16[256,2048]{1,0:T(8,128)(2,1)} async-done(((bf16[2048,2048]{1,0:T(8,128)(2,1)}), bf16[256,2048]{1,0:T(8,128)(2,1)}) %reduce-scatter.11.cloned.1.call-update) | async-done | bytes 1048592 | tf_op jit(solution)/shard_map/reduce_scatter | solution.py:157
  239.6 53.8 %all-gather.7.cloned.1.call-done = bf16[2048,2048]{1,0:T(8,128)(2,1)} async-done(((bf16[256,2048]{1,0:T(8,128)(2,1)}), bf16[2048,2048]{1,0:T(8,128)(2,1)}) %all-gather.7.cloned.1.call-update) | async-done | bytes 8388624 | tf_op jit(solution)/shard_map/all_gather | solution.py:164
  293.4 18.8 %fusion.53 = f32[2048,2,704]{0,2,1:T(8,128)} fusion(bf16[2048,2048]{1,0:T(8,128)(2,1)} %all-gather.7.cloned.1.call-done, bf16[2048,2,704]{0,2,1:T(8,128)(2,1)} %param.23), kind=kOutput, calls=%fused_computation.64 | convolution fusion | flops 11811160064 | bytes 25690112 | tf_op jit(solution)/shard_map/dot_general | solution.py:165
  312.2 37.2 %all-gather.9.cloned.1.call-done = bf16[2048,2048]{1,0:T(8,128)(2,1)} async-done(((bf16[256,2048]{1,0:T(8,128)(2,1)}), bf16[2048,2048]{1,0:T(8,128)(2,1)}) %all-gather.9.cloned.1.call-update) | async-done | bytes 8388624 | tf_op jit(solution)/shard_map/all_gather | solution.py:180
  349.4 12.9 multiply_bitcast_fusion.1
  364.9 17.9 %bitcast_convert_fusion = bf16[2048,2048]{1,0:T(8,128)(2,1)} fusion(bf16[2048,2,704]{0,2,1:T(8,128)(2,1)} %param.23, bf16[2048,1,704]{0,2,1:T(8,128)(2,1)S(1)} %get-tuple-element.303, bf16[2048,1,704]{0,2,1:T(8,128)(2,1)S(1)} %get-tuple-element.302), kind=kOutput, calls=%fused_computation.56 | convolution fusion | flops 11818237952 | bytes 19922944 | tf_op jit(solution)/shard_map/dot_general | solution.py:81
  382.8 71.6 %reduce-scatter.15.cloned.1.call-done = bf16[256,2048]{1,0:T(8,128)(2,1)} async-done(((bf16[2048,2048]{1,0:T(8,128)(2,1)}), bf16[256,2048]{1,0:T(8,128)(2,1)}) %reduce-scatter.15.cloned.1.call-update) | async-done | bytes 1048592 | tf_op jit(solution)/shard_map/reduce_scatter | solution.py:192
  461.6 54.3 %all-gather.11.cloned.1.call-done = bf16[2048,2048]{1,0:T(8,128)(2,1)} async-done(((bf16[256,2048]{1,0:T(8,128)(2,1)}), bf16[2048,2048]{1,0:T(8,128)(2,1)}) %all-gather.11.cloned.1.call-update) | async-done | bytes 8388624 | tf_op jit(solution)/shard_map/all_gather | solution.py:202
  515.9 7.0 convolution_convert_fusion.5
  531.4 245.9 %while.29 = (s32[]{:T(128)}, f32[2048,4,64]{0,2,1:T(8,128)}, f32[2048,4,64]{0,2,1:T(8,128)}, f32[4,512,4,64]{1,0,3,2:T(4,128)}, bf16[4,512,4,64]{1,3,2,0:T(8,128...) while((s32[]{:T(128)}, f32[2048,4,64]{0,2,1:T(8,128)}, ...), condition=%wide.region_17.18_spmd.clone, body=%wide.region_15.17_spmd.clone.sunk | while | flops 2753165312 | bytes 233386272 | solution.py:238
  536.5 5.7 copy-done.1
  542.2 7.1 fusion.163
  549.3 12.8 multiply_reduce_fusion.3
  562.1 12.2 multiply_convert_fusion.3
  581.5 11.1 dynamic_update_slice.22
  603.3 7.5 fusion.163
  610.8 12.8 multiply_reduce_fusion.3
  623.6 12.2 multiply_convert_fusion.3
  643.0 11.1 dynamic_update_slice.22
  664.8 7.5 fusion.163
  672.3 12.8 multiply_reduce_fusion.3
  685.1 12.2 multiply_convert_fusion.3
  704.5 11.1 dynamic_update_slice.22
  726.3 7.5 fusion.163
  733.8 12.8 multiply_reduce_fusion.3
  746.6 12.2 multiply_convert_fusion.3
  766.0 11.1 dynamic_update_slice.22
  788.6 9.2 convolution_convert_fusion
  804.6 9.1 convolution_convert_fusion.1
  813.8 11.4 convolution_convert_fusion.3
  825.2 16.2 %fusion.58 = bf16[2048,2,704]{0,2,1:T(8,128)(2,1)} fusion(bf16[2048,2048]{1,0:T(8,128)(2,1)} %all-gather.7.cloned.1.call-done, bf16[2048,1,704]{0,2,1:T(8,128)(2,1)S(1)} %copy-done.47, bf16[2048,1,704]{0,2,1:T(8,128)(2,1)S(1)} %copy-done.45), kind=kOutput, calls=%fused_computation.79 | convolution fusion | flops 11825577984 | bytes 19922944 | tf_op jit(solution)/shard_map/dot_general | solution.py:75
  842.9 11.6 fusion.66
  854.5 14.9 %reduce-scatter.17.cloned.1.call-done = bf16[256,2048]{1,0:T(8,128)(2,1)} async-done(((bf16[2048,2048]{1,0:T(8,128)(2,1)}), bf16[256,2048]{1,0:T(8,128)(2,1)}) %reduce-scatter.17.cloned.1.call-update) | async-done | bytes 1048592 | tf_op jit(solution)/shard_map/reduce_scatter | solution.py:257
  875.7 7.5 convolution_convert_fusion.4
  883.5 61.5 %reduce-scatter.13.cloned.1.call-done = bf16[256,2048]{1,0:T(8,128)(2,1)} async-done(((bf16[2048,2048]{1,0:T(8,128)(2,1)}), bf16[256,2048]{1,0:T(8,128)(2,1)}) %reduce-scatter.13.cloned.1.call-update) | async-done | bytes 1048592 | tf_op jit(solution)/shard_map/reduce_scatter | solution.py:173
  950.3 32.5 %reduce-scatter.19.cloned.1.call-done = bf16[256,2]{1,0:T(8,128)(2,1)} async-done(((bf16[2048,2]{1,0:T(8,128)(2,1)}), bf16[256,2]{1,0:T(8,128)(2,1)}) %reduce-scatter.19.cloned.1.call-update) | async-done | bytes 1040
  983.7 36.2 %reduce-scatter.21.cloned.1.call-done = bf16[256,2]{1,0:T(8,128)(2,1)} async-done(((bf16[2048,2]{1,0:T(8,128)(2,1)}), bf16[256,2]{1,0:T(8,128)(2,1)}) %reduce-scatter.21.cloned.1.call-update) | async-done | bytes 1040
  1020.8 11.9 all-reduce.1
  1035.0 423.0 %all-reduce.5.cloned.1.call-done = (bf16[2048,3,256]{2,0,1:T(8,128)(2,1)}, bf16[256,2048]{1,0:T(8,128)(2,1)}, bf16[2048,2,704]{0,2,1:T(8,128)(2,1)}, bf16[704,2048]{1,0:T(8,128)(2,1)}) async-done(((bf16[2048,3,256]{2,0,1:T(8,128)(2,1)}, bf16[256,2048]{1,0:T(8,128)(2,1)}, bf16[2048,2,704]{0,2,1:T(8,128)(2,1)}, bf16[704,2048]{1,0:T(8,128)(2,1)}), (bf16[2048,3,256]{2,0,1:T(8,128)(2,1)}, ...) | async-done | bytes 12845072 | tf_op jit(solution)/shard_map/psum | solution.py:282
  1468.0 6.0 convert_element_type.171
  (287 shorter events, 200.0 us)
Async XLA Ops:
  7.2 342.3 %copy-start = (bf16[704,2048]{1,0:T(8,128)(2,1)S(1)}, bf16[704,2048]{1,0:T(8,128)(2,1)}, u32[]{:S(2)}) copy-start(bf16[704,2048]{1,0:T(8,128)(2,1)} %param.24) | copy-start | bytes 8650756
  7.2 8.9 copy-start.42
  7.2 9.6 copy-start.18
  7.2 66.0 %all-gather.5.cloned.1.call-start = ((), (), s32[]{:S(2)}) async-start(), calls=%async_computation.6 | async-start | bytes 9437184 | tf_op jit(solution)/shard_map/all_gather | solution.py:113
  8.9 4.5 copy-start.31
  16.0 217.2 %reduce-scatter.11.cloned.1.call-start = ((), (), s32[]{:S(2)}) async-start(), calls=%async_computation.7 | async-start | bytes 9437184 | tf_op jit(solution)/shard_map/reduce_scatter | solution.py:157
  18.1 4.7 copy-start.43
  23.3 61.6 %copy-start.20 = (f32[2048,8]{0,1:T(8,128)}, f32[2048,8]{0,1:T(8,128)S(1)}, u32[]{:S(2)}) copy-start(f32[2048,8]{0,1:T(8,128)S(1)} %get-tuple-element.324) | copy-start | bytes 196612
  23.3 61.6 %copy-start.22 = (f32[2048,8]{0,1:T(8,128)}, f32[2048,8]{0,1:T(8,128)S(1)}, u32[]{:S(2)}) copy-start(f32[2048,8]{0,1:T(8,128)S(1)} %get-tuple-element.325) | copy-start | bytes 196612
  94.1 4.3 copy-start.7
  110.1 4.3 copy-start.7
  141.9 4.3 copy-start.7
  161.6 75.8 %copy-start.24 = (f32[1,2048]{1,0:T(1,128)S(1)}, f32[1,2048]{1,0:T(1,128)}, u32[]{:S(2)}) copy-start(f32[1,2048]{1,0:T(1,128)} %get-tuple-element.321) | copy-start | bytes 24580
  161.6 75.8 %copy-start.30 = (f32[1,2048]{1,0:T(1,128)S(1)}, f32[1,2048]{1,0:T(1,128)}, u32[]{:S(2)}) copy-start(f32[1,2048]{1,0:T(1,128)} %get-tuple-element.323) | copy-start | bytes 24580
  161.7 131.7 %all-gather.7.cloned.1.call-start = ((), (), s32[]{:S(2)}) async-start(), calls=%async_computation.8 | async-start | bytes 9437184 | tf_op jit(solution)/shard_map/all_gather | solution.py:164
  235.3 222.7 %copy-start.28 = (f32[256]{0:T(256)}, f32[256]{0:T(256)S(1)}, u32[]{:S(2)}) copy-start(f32[256]{0:T(256)S(1)} %broadcast_multiply_fusion.4) | copy-start | bytes 3076
  237.4 220.7 %copy-start.33 = (f32[256]{0:T(256)}, f32[256]{0:T(256)S(1)}, u32[]{:S(2)}) copy-start(f32[256]{0:T(256)S(1)} %add_rsqrt_fusion) | copy-start | bytes 3076
  239.0 110.4 %all-gather.9.cloned.1.call-start = ((), (), s32[]{:S(2)}) async-start(), calls=%async_computation.10 | async-start | bytes 9437184 | tf_op jit(solution)/shard_map/all_gather | solution.py:180
  239.6 214.8 %reduce-scatter.15.cloned.1.call-start = ((), (), s32[]{:S(2)}) async-start(), calls=%async_computation.11 | async-start | bytes 9437184 | tf_op jit(solution)/shard_map/reduce_scatter | solution.py:192
  382.8 133.1 %all-gather.11.cloned.1.call-start = ((), (), s32[]{:S(2)}) async-start(), calls=%async_computation.12 | async-start | bytes 9437184 | tf_op jit(solution)/shard_map/all_gather | solution.py:202
  461.5 407.9 %reduce-scatter.17.cloned.1.call-start = ((), (), s32[]{:S(2)}) async-start(), calls=%async_computation.13 | async-start | bytes 9437184 | tf_op jit(solution)/shard_map/reduce_scatter | solution.py:257
  536.4 5.7 copy-start.1
  562.1 12.2 copy-start.2
  597.5 5.7 copy-start.1
  623.6 12.2 copy-start.2
  659.0 5.7 copy-start.1
  685.1 12.2 copy-start.2
  720.5 5.7 copy-start.1
  746.5 12.2 copy-start.2
  777.3 5.2 copy-start.21
  777.3 5.2 copy-start.23
  797.8 147.2 %reduce-scatter.13.cloned.1.call-start = ((), (), s32[]{:S(2)}) async-start(), calls=%async_computation.9 | async-start | bytes 9437184 | tf_op jit(solution)/shard_map/reduce_scatter | solution.py:173
  813.7 169.1 %reduce-scatter.19.cloned.1.call-start = ((), (), s32[]{:S(2)}) async-start(), calls=%async_computation.14 | async-start | bytes 589824
  813.8 11.4 copy-start.45
  813.8 11.4 copy-start.47
  825.2 17.6 %copy-start.37 = (bf16[2048]{0:T(1024)(128)(2,1)S(1)}, bf16[2048]{0:T(1024)(128)(2,1)}, u32[]{:S(2)}) copy-start(bf16[2048]{0:T(1024)(128)(2,1)} %get-tuple-element.234) | copy-start | bytes 12292
  842.9 28.0 %copy-start.27 = (f32[1,2048]{1,0:T(1,128)S(1)}, f32[1,2048]{1,0:T(1,128)}, u32[]{:S(2)}) copy-start(f32[1,2048]{1,0:T(1,128)} %copy-done.26) | copy-start | bytes 24580
  842.9 28.0 %copy-start.32 = (f32[256]{0:T(256)S(1)}, f32[256]{0:T(256)}, u32[]{:S(2)}) copy-start(f32[256]{0:T(256)} %copy-done.31) | copy-start | bytes 3076
  842.9 28.0 %copy-start.36 = (f32[256]{0:T(256)S(1)}, f32[256]{0:T(256)}, u32[]{:S(2)}) copy-start(f32[256]{0:T(256)} %copy-done.35) | copy-start | bytes 3076
  874.5 145.4 %reduce-scatter.21.cloned.1.call-start = ((), (), s32[]{:S(2)}) async-start(), calls=%async_computation.15 | async-start | bytes 589824
  875.6 582.3 %all-reduce.5.cloned.1.call-start = ((), (), s32[]{:S(2)}) async-start(), calls=%async_computation.16 | async-start | bytes 25690112 | tf_op jit(solution)/shard_map/psum | solution.py:282
  883.2 61.7 %copy-start.25 = (f32[1,2048]{1,0:T(1,128)S(1)}, f32[1,2048]{1,0:T(1,128)}, u32[]{:S(2)}) copy-start(f32[1,2048]{1,0:T(1,128)} %get-tuple-element.321) | copy-start | bytes 24580
  883.2 61.7 %copy-start.29 = (f32[256]{0:T(256)S(1)}, f32[256]{0:T(256)}, u32[]{:S(2)}) copy-start(f32[256]{0:T(256)} %copy-done.28) | copy-start | bytes 3076
  883.2 61.7 %copy-start.34 = (f32[256]{0:T(256)S(1)}, f32[256]{0:T(256)}, u32[]{:S(2)}) copy-start(f32[256]{0:T(256)} %copy-done.33) | copy-start | bytes 3076
  883.2 61.7 %copy-start.39 = (f32[256]{0:T(256)S(1)}, f32[256]{0:T(256)}, u32[]{:S(2)}) copy-start(f32[256]{0:T(256)} %copy-done.38) | copy-start | bytes 3076
  883.2 61.7 %copy-start.41 = (f32[256]{0:T(256)S(1)}, f32[256]{0:T(256)}, u32[]{:S(2)}) copy-start(f32[256]{0:T(256)} %copy-done.40) | copy-start | bytes 3076
  1458.0 10.0 slice-start
  1460.9 7.1 slice-start.1
  (28 other events, 74.0 us)
Sparse Core Ops, SparseCore 0:
  16.2 56.9 all-gather.4
  161.8 71.4 reduce-scatter.10
  239.1 54.2 all-gather.6
  295.1 54.2 all-gather.8
  382.9 71.4 reduce-scatter.14
  461.6 54.2 all-gather.10
  797.9 71.4 reduce-scatter.16
  873.4 71.4 reduce-scatter.12
  948.6 34.1 reduce-scatter.18
  985.7 34.1 reduce-scatter.20
  1023.3 434.5 all-reduce.4
where the time goes:
time: 1490 us; the launch traced here: 1480 us
  waiting for transfers between devices  907 us (61%)
  matrix products  296 us (20%)
  other arithmetic  133 us (9%)
  local copies, waits for them, and re-layouts  116 us (8%)
    psum x1, waiting for transfers between devices, local(): lax.psum(grad_qkv.astype(jnp.bfloat16), 'dp').astype(jnp.float32)  423 us
    reduce_scatter x1, waiting for transfers between devices, local(): lax.psum_scatter(contract_cols(grad_pair, gate_matrix).astype(jnp.bfloat1...  71.6 us
    reduce_scatter x1, waiting for transfers between devices, local(): lax.psum_scatter(jnp.dot(attended, w_out, preferred_element_type=jnp.floa...  71.6 us
    unnamed x13, waiting for transfers between devices  69.3 us
    reduce_scatter x1, waiting for transfers between devices, local(): lax.psum_scatter(jnp.dot(activation, w_down, preferred_element_type=jnp.f...  61.5 us
    all_gather x1, waiting for transfers between devices, local(): lax.all_gather(grad_hidden.astype(jnp.bfloat16), 'tp', axis=0, tiled=True)  54.3 us
    all_gather x1, waiting for transfers between devices, local(): lax.all_gather(normed_two.astype(jnp.bfloat16), 'tp', axis=0, tiled=True)  53.8 us
    dot_general x4, matrix products, backward_block(): jnp.einsum('bhd,khd->hbk', grad_block, value_rows, preferred_element_type...  51.2 us
  transfers between devices with their start and end apart: 11, of which 11 were waited for; matrix products, arithmetic and copies ran while one was open for 7% of the time, Pallas kernels for 0%

commit v1 on v0

--- a/solution.py
+++ b/solution.py
@@ -8,6 +8,28 @@
 HEAD_DIM = 64
 ROT = 16
 EPSILON = 1e-05
+
+
+def in_order(blocks, dim):
+    blocks = jnp.moveaxis(blocks, 0, dim)
+    lengths = blocks.shape
+    return blocks.reshape(*lengths[:dim], lengths[dim] * lengths[dim + 1], *lengths[dim + 2 :])
+
+
+def ring_gather(x, axis, dim):
+    peers = lax.axis_size(axis)
+    pairs = [(i, (i + 1) % peers) for i in range(peers)]
+    back = [(b, a) for a, b in pairs]
+    lower, upper = ([], [])
+    for step in range(peers - 1):
+        if step % 2 == 0:
+            lower.append(lax.ppermute(lower[-1] if lower else x, axis, pairs))
+        else:
+            upper.append(lax.ppermute(upper[-1] if upper else x, axis, back))
+    parts = jnp.stack([*lower[::-1], x, *upper])
+    shift = lax.axis_index(axis) - len(lower)
+    parts = parts[(jnp.arange(peers) - shift) % peers]
+    return in_order(parts, dim)
 
 
 def norm_forward(values, gain, shift_bias):
@@ -177,7 +199,7 @@
         tiled=True,
     ).astype(jnp.float32)
     grad_float = out_grad.astype(jnp.float32)
-    portion = lax.all_gather(out_grad, "tp", axis=0, tiled=True)
+    portion = ring_gather(out_grad, "tp", 0)
     weight_sum = contract_rows(activation, portion)
     grad_act = contract_cols(portion, w_down)
     grad_down, grad_act = (weight_sum, grad_act)

time: 1490 us -> 1540 us (1.034)
  local copies, waits for them, and re-layouts: 116 us -> 137 us
  waiting for transfers between devices: 907 us -> 925 us
    ppermute x0 -> x7, waiting for transfers between devices: none -> 109 us  [the longest x4 109 us: ring_gather(): lower.append(lax.ppermute(lower[-1] if lower else x, axis, pairs))]
    all_gather x1, waiting for transfers between devices: 53.8 us -> 0.01 us  [local(): lax.all_gather(normed_two.astype(jnp.bfloat16), 'tp', axis=0, tiled=True)]
    all_gather x1 -> x0, waiting for transfers between devices: 37.2 us -> none  [local(): portion = lax.all_gather(out_grad, 'tp', axis=0, tiled=True)]
    unnamed x100 -> x113, local copies, waits for them, and re-layouts: 22.1 us -> 33.6 us
    unnamed x13 -> x12, waiting for transfers between devices: 69.3 us -> 68.9 us
  transfers between devices with their start and end apart: 11 -> 17, of which waited for: 11 -> 14; matrix products, arithmetic and copies ran while one was open for 7% -> 7% of each run, Pallas kernels for 0% -> 0%
where the time goes in v1:
time: 1540 us; the launch traced here: 1530 us
  waiting for transfers between devices  925 us (60%)
  matrix products  303 us (20%)
  local copies, waits for them, and re-layouts  137 us (9%)
  other arithmetic  129 us (8%)
    psum x1, waiting for transfers between devices, local(): lax.psum(grad_qkv.astype(jnp.bfloat16), 'dp').astype(jnp.float32)  423 us
    ppermute x4, waiting for transfers between devices, ring_gather(): lower.append(lax.ppermute(lower[-1] if lower else x, axis, pairs))  109 us
    reduce_scatter x1, waiting for transfers between devices, local(): lax.psum_scatter(contract_cols(grad_pair, gate_matrix).astype(jnp.bfloat1...  73.1 us
    reduce_scatter x1, waiting for transfers between devices, local(): lax.psum_scatter(jnp.dot(attended, w_out, preferred_element_type=jnp.floa...  71.6 us
    unnamed x12, waiting for transfers between devices  68.9 us
    reduce_scatter x1, waiting for transfers between devices, local(): lax.psum_scatter(jnp.dot(activation, w_down, preferred_element_type=jnp.f...  60.7 us
    all_gather x1, waiting for transfers between devices, local(): lax.all_gather(grad_hidden.astype(jnp.bfloat16), 'tp', axis=0, tiled=True)  54.3 us
    dot_general x4, matrix products, backward_block(): jnp.einsum('bhd,khd->hbk', grad_block, value_rows, preferred_element_type...  51.3 us
  transfers between devices with their start and end apart: 17, of which 14 were waited for; matrix products, arithmetic and copies ran while one was open for 7% of the time, Pallas kernels for 0%

profile of v1, /device:TPU:0, one launch (start us, length us, event | category | flops | bytes accessed | tf_op | source)
XLA Modules:
  0.0 1532.0 jit_solution(3001224195510212642)
XLA Ops:
  23.3 49.9 %all-gather.4.cloned.1.call-done = bf16[2048,2048]{1,0:T(8,128)(2,1)} async-done(((bf16[256,2048]{1,0:T(8,128)(2,1)}), bf16[2048,2048]{1,0:T(8,128)(2,1)}) %all-gather.4.cloned.1.call-update) | async-done | bytes 8388624 | tf_op jit(solution)/shard_map/all_gather | solution.py:135
  73.2 10.1 fusion.70
  88.5 63.9 %while.28 = (s32[]{:T(128)}, bf16[4,512,4,64]{1,3,2,0:T(8,128)(2,1)}, f32[4,4,512]{2,1,0:T(4,128)S(1)}, s32[4,512]{1,0:T(4,128)S(1)}, s32[1,2048]{1,0:T(1,128)S(...) while((s32[]{:T(128)}, ...), condition=%wide.region_7.8_spmd.clone, body=%wide.region_4.7_spmd.clone.sunk | while | flops 1127348224 | bytes 61427864 | solution.py:177
  98.4 5.9 fusion.161
  114.4 5.9 fusion.161
  146.2 5.9 fusion.161
  161.6 71.6 %reduce-scatter.11.cloned.1.call-done = bf16[256,2048]{1,0:T(8,128)(2,1)} async-done(((bf16[2048,2048]{1,0:T(8,128)(2,1)}), bf16[256,2048]{1,0:T(8,128)(2,1)}) %reduce-scatter.11.cloned.1.call-update) | async-done | bytes 1048592 | tf_op jit(solution)/shard_map/reduce_scatter | solution.py:179
  239.1 23.0 %collective-permute-done = bf16[256,2048]{1,0:T(8,128)(2,1)S(1)} collective-permute-done((bf16[256,2048]{1,0:T(8,128)(2,1)}, bf16[256,2048]{1,0:T(8,128)(2,1)S(1)}, u32[]{:S(2)}, u32[]{:S(2)}) %collective-permute-start) | collective-permute-done | bytes 1048608 | tf_op jit(solution)/shard_map/ppermute | solution.py:26
  265.7 38.6 %collective-permute-done.1 = bf16[256,2048]{1,0:T(8,128)(2,1)S(1)} collective-permute-done((bf16[256,2048]{1,0:T(8,128)(2,1)S(1)}, bf16[256,2048]{1,0:T(8,128)(2,1)S(1)}, u32[]{:S(2)}, u32[]{:S(2)}) %collective-permute-start.1) | collective-permute-done | bytes 1048608 | tf_op jit(solution)/shard_map/ppermute | solution.py:26
  310.3 24.2 %collective-permute-done.2 = bf16[256,2048]{1,0:T(8,128)(2,1)} collective-permute-done((bf16[256,2048]{1,0:T(8,128)(2,1)S(1)}, bf16[256,2048]{1,0:T(8,128)(2,1)}, u32[]{:S(2)}, u32[]{:S(2)}) %collective-permute-start.2) | collective-permute-done | bytes 1048608 | tf_op jit(solution)/shard_map/ppermute | solution.py:26
  337.2 23.1 %collective-permute-done.3 = bf16[256,2048]{1,0:T(8,128)(2,1)} collective-permute-done((bf16[256,2048]{1,0:T(8,128)(2,1)}, bf16[256,2048]{1,0:T(8,128)(2,1)}, u32[]{:S(2)}, u32[]{:S(2)}) %collective-permute-start.3) | collective-permute-done | bytes 1048608 | tf_op jit(solution)/shard_map/ppermute | solution.py:26
  373.7 8.3 gather_fusion
  382.0 19.0 %fusion.53 = f32[2048,2,704]{0,2,1:T(8,128)} fusion(bf16[2048,2048]{1,0:T(8,128)(2,1)} %all-gather.6.cloned.1.call-done, bf16[2048,2,704]{0,2,1:T(8,128)(2,1)} %param.23), kind=kOutput, calls=%fused_computation.65 | convolution fusion | flops 11811160064 | bytes 25690112 | tf_op jit(solution)/shard_map/dot_general | solution.py:187
  400.9 12.2 fusion.60
  414.8 17.6 %bitcast_convert_fusion = bf16[2048,2048]{1,0:T(8,128)(2,1)} fusion(bf16[2048,2,704]{0,2,1:T(8,128)(2,1)S(1)} %bitcast.303, bf16[2048,1,704]{0,2,1:T(8,128)(2,1)} %get-tuple-element.303, bf16[2048,1,704]{0,2,1:T(8,128)(2,1)S(1)} %get-tuple-element.302), kind=kOutput, calls=%fused_computation.57 | convolution fusion | flops 11818237952 | bytes 19922944 | tf_op jit(solution)/shard_map/dot_general | solution.py:103
  432.5 73.1 %reduce-scatter.15.cloned.1.call-done = bf16[256,2048]{1,0:T(8,128)(2,1)} async-done(((bf16[2048,2048]{1,0:T(8,128)(2,1)}), bf16[256,2048]{1,0:T(8,128)(2,1)}) %reduce-scatter.15.cloned.1.call-update) | async-done | bytes 1048592 | tf_op jit(solution)/shard_map/reduce_scatter | solution.py:214
  513.5 54.3 %all-gather.8.cloned.1.call-done = bf16[2048,2048]{1,0:T(8,128)(2,1)} async-done(((bf16[256,2048]{1,0:T(8,128)(2,1)}), bf16[2048,2048]{1,0:T(8,128)(2,1)}) %all-gather.8.cloned.1.call-update) | async-done | bytes 8388624 | tf_op jit(solution)/shard_map/all_gather | solution.py:224
  567.8 7.0 convolution_convert_fusion.5
  583.3 246.0 %while.29 = (s32[]{:T(128)}, f32[2048,4,64]{0,2,1:T(8,128)}, f32[2048,4,64]{0,2,1:T(8,128)}, f32[4,512,4,64]{1,0,3,2:T(4,128)}, bf16[4,512,4,64]{1,3,2,0:T(8,128...) while((s32[]{:T(128)}, f32[2048,4,64]{0,2,1:T(8,128)}, ...), condition=%wide.region_17.18_spmd.clone, body=%wide.region_15.17_spmd.clone.sunk | while | flops 2753165312 | bytes 233386272 | solution.py:260
  594.1 7.1 fusion.174
  601.2 12.8 multiply_reduce_fusion.3
  614.0 12.2 multiply_convert_fusion.4
  633.5 11.1 dynamic_update_slice.22
  655.2 7.5 fusion.174
  662.7 12.8 multiply_reduce_fusion.3
  675.5 12.2 multiply_convert_fusion.4
  695.0 11.1 dynamic_update_slice.22
  716.7 7.5 fusion.174
  724.2 12.8 multiply_reduce_fusion.3
  737.0 12.2 multiply_convert_fusion.4
  756.5 11.1 dynamic_update_slice.22
  778.2 7.5 fusion.174
  785.7 12.8 multiply_reduce_fusion.3
  798.5 12.2 multiply_convert_fusion.4
  818.0 11.1 dynamic_update_slice.22
  840.2 9.1 convolution_convert_fusion
  849.4 13.8 convolution_convert_fusion.1
  863.3 14.1 convolution_convert_fusion.3
  877.4 16.2 %fusion.65 = bf16[2048,2,704]{0,2,1:T(8,128)(2,1)} fusion(bf16[2048,2048]{1,0:T(8,128)(2,1)} %all-gather.6.cloned.1.call-done, bf16[2048,1,704]{0,2,1:T(8,128)(2,1)S(1)} %copy-done.48, bf16[2048,1,704]{0,2,1:T(8,128)(2,1)S(1)} %copy-done.47), kind=kOutput, calls=%fused_computation.88 | convolution fusion | flops 11825577984 | bytes 19922944 | tf_op jit(solution)/shard_map/dot_general | solution.py:97
  895.1 11.5 fusion.73
  906.7 14.4 reduce-scatter.17.cloned.1.call-done
  927.3 7.7 convolution_convert_fusion.4
  935.3 60.7 %reduce-scatter.13.cloned.1.call-done = bf16[256,2048]{1,0:T(8,128)(2,1)} async-done(((bf16[2048,2048]{1,0:T(8,128)(2,1)}), bf16[256,2048]{1,0:T(8,128)(2,1)}) %reduce-scatter.13.cloned.1.call-update) | async-done | bytes 1048592 | tf_op jit(solution)/shard_map/reduce_scatter | solution.py:195
  1001.4 32.4 %reduce-scatter.19.cloned.1.call-done = bf16[256,2]{1,0:T(8,128)(2,1)} async-done(((bf16[2048,2]{1,0:T(8,128)(2,1)}), bf16[256,2]{1,0:T(8,128)(2,1)}) %reduce-scatter.19.cloned.1.call-update) | async-done | bytes 1040
  1034.7 36.3 %reduce-scatter.21.cloned.1.call-done = bf16[256,2]{1,0:T(8,128)(2,1)} async-done(((bf16[2048,2]{1,0:T(8,128)(2,1)}), bf16[256,2]{1,0:T(8,128)(2,1)}) %reduce-scatter.21.cloned.1.call-update) | async-done | bytes 1040
  1071.9 11.9 all-reduce.1
  1086.2 422.8 %all-reduce.5.cloned.1.call-done = (bf16[2048,3,256]{2,0,1:T(8,128)(2,1)}, bf16[256,2048]{1,0:T(8,128)(2,1)}, bf16[2048,2,704]{0,2,1:T(8,128)(2,1)}, bf16[704,2048]{1,0:T(8,128)(2,1)}) async-done(((bf16[2048,3,256]{2,0,1:T(8,128)(2,1)}, bf16[256,2048]{1,0:T(8,128)(2,1)}, bf16[2048,2,704]{0,2,1:T(8,128)(2,1)}, bf16[704,2048]{1,0:T(8,128)(2,1)}), (bf16[2048,3,256]{2,0,1:T(8,128)(2,1)}, ...) | async-done | bytes 12845072 | tf_op jit(solution)/shard_map/psum | solution.py:304
  1519.0 6.0 convert_element_type.176
  (315 shorter events, 235.3 us)
Async XLA Ops:
  7.2 393.8 %copy-start = (bf16[704,2048]{1,0:T(8,128)(2,1)S(1)}, bf16[704,2048]{1,0:T(8,128)(2,1)}, u32[]{:S(2)}) copy-start(bf16[704,2048]{1,0:T(8,128)(2,1)} %param.24) | copy-start | bytes 8650756
  7.2 66.0 %all-gather.4.cloned.1.call-start = ((), (), s32[]{:S(2)}) async-start(), calls=%async_computation.6 | async-start | bytes 9437184 | tf_op jit(solution)/shard_map/all_gather | solution.py:135
  16.0 217.2 %reduce-scatter.11.cloned.1.call-start = ((), (), s32[]{:S(2)}) async-start(), calls=%async_computation.7 | async-start | bytes 9437184 | tf_op jit(solution)/shard_map/reduce_scatter | solution.py:179
  23.3 61.6 %copy-start.22 = (f32[2048,8]{0,1:T(8,128)}, f32[2048,8]{0,1:T(8,128)S(1)}, u32[]{:S(2)}) copy-start(f32[2048,8]{0,1:T(8,128)S(1)} %get-tuple-element.324) | copy-start | bytes 196612
  23.3 61.6 %copy-start.24 = (f32[2048,8]{0,1:T(8,128)}, f32[2048,8]{0,1:T(8,128)S(1)}, u32[]{:S(2)}) copy-start(f32[2048,8]{0,1:T(8,128)S(1)} %get-tuple-element.325) | copy-start | bytes 196612
  161.6 75.8 %copy-start.26 = (f32[1,2048]{1,0:T(1,128)S(1)}, f32[1,2048]{1,0:T(1,128)}, u32[]{:S(2)}) copy-start(f32[1,2048]{1,0:T(1,128)} %get-tuple-element.321) | copy-start | bytes 24580
  161.6 75.8 %copy-start.32 = (f32[1,2048]{1,0:T(1,128)S(1)}, f32[1,2048]{1,0:T(1,128)}, u32[]{:S(2)}) copy-start(f32[1,2048]{1,0:T(1,128)} %get-tuple-element.323) | copy-start | bytes 24580
  161.6 220.4 %all-gather.6.cloned.1.call-start = ((), (), s32[]{:S(2)}) async-start(), calls=%async_computation.8 | async-start | bytes 9437184 | tf_op jit(solution)/shard_map/all_gather | solution.py:186
  235.3 273.8 %copy-start.30 = (f32[256]{0:T(256)}, f32[256]{0:T(256)S(1)}, u32[]{:S(2)}) copy-start(f32[256]{0:T(256)S(1)} %broadcast_multiply_fusion.4) | copy-start | bytes 3076
  237.3 271.8 %copy-start.35 = (f32[256]{0:T(256)}, f32[256]{0:T(256)S(1)}, u32[]{:S(2)}) copy-start(f32[256]{0:T(256)S(1)} %add_rsqrt_fusion) | copy-start | bytes 3076
  238.9 266.7 %reduce-scatter.15.cloned.1.call-start = ((), (), s32[]{:S(2)}) async-start(), calls=%async_computation.10 | async-start | bytes 9437184 | tf_op jit(solution)/shard_map/reduce_scatter | solution.py:214
  239.0 23.1 %collective-permute-start = (bf16[256,2048]{1,0:T(8,128)(2,1)}, bf16[256,2048]{1,0:T(8,128)(2,1)S(1)}, u32[]{:S(2)}, u32[]{:S(2)}) collective-permute-start(bf16[256,2048]{1,0:T(8,128)(2,1)} %param.25), channel_id=1, source_target_pairs={{0,1},{1,2},{2,3},{3,4},{4,5},{5,6},{6,7},{7,0},{8,9},{9,10},{10,1... | collective-permute-start | bytes 3145736 | tf_op jit(solution)/shard_map/ppermute | solution.py:26
  263.1 41.3 %collective-permute-start.1 = (bf16[256,2048]{1,0:T(8,128)(2,1)S(1)}, bf16[256,2048]{1,0:T(8,128)(2,1)S(1)}, u32[]{:S(2)}, u32[]{:S(2)}) collective-permute-start(bf16[256,2048]{1,0:T(8,128)(2,1)S(1)} %collective-permute-done), channel_id=1, source_target_pairs={{0,1},{1,2},{2,3},{3,4},{4,5},{5,6},{6,7},{7,0},{8,9},{9,10},{10,1... | collective-permute-start | bytes 3145736 | tf_op jit(solution)/shard_map/ppermute | solution.py:26
  263.7 43.7 %collective-permute-start.4 = (bf16[256,2048]{1,0:T(8,128)(2,1)}, bf16[256,2048]{1,0:T(8,128)(2,1)}, u32[]{:S(2)}, u32[]{:S(2)}) collective-permute-start(bf16[256,2048]{1,0:T(8,128)(2,1)} %param.25), channel_id=1, source_target_pairs={{1,0},{2,1},{3,2},{4,3},{5,4},{6,5},{7,6},{0,7},{9,8},{10,9},{11,1... | collective-permute-start | bytes 3145736 | tf_op jit(solution)/shard_map/ppermute | solution.py:28
  305.3 29.2 %collective-permute-start.2 = (bf16[256,2048]{1,0:T(8,128)(2,1)S(1)}, bf16[256,2048]{1,0:T(8,128)(2,1)}, u32[]{:S(2)}, u32[]{:S(2)}) collective-permute-start(bf16[256,2048]{1,0:T(8,128)(2,1)S(1)} %collective-permute-done.1), channel_id=1, source_target_pairs={{0,1},{1,2},{2,3},{3,4},{4,5},{5,6},{6,7},{7,0},{8,9},{9,10},{10,1... | collective-permute-start | bytes 3145736 | tf_op jit(solution)/shard_map/ppermute | solution.py:26
  307.5 27.0 %collective-permute-start.5 = (bf16[256,2048]{1,0:T(8,128)(2,1)}, bf16[256,2048]{1,0:T(8,128)(2,1)}, u32[]{:S(2)}, u32[]{:S(2)}) collective-permute-start(bf16[256,2048]{1,0:T(8,128)(2,1)} %collective-permute-done.4), channel_id=1, source_target_pairs={{1,0},{2,1},{3,2},{4,3},{5,4},{6,5},{7,6},{0,7},{9,8},{10,9},{11,1... | collective-permute-start | bytes 3145736 | tf_op jit(solution)/shard_map/ppermute | solution.py:28
  334.5 25.9 %collective-permute-start.3 = (bf16[256,2048]{1,0:T(8,128)(2,1)}, bf16[256,2048]{1,0:T(8,128)(2,1)}, u32[]{:S(2)}, u32[]{:S(2)}) collective-permute-start(bf16[256,2048]{1,0:T(8,128)(2,1)} %collective-permute-done.2), channel_id=1, source_target_pairs={{0,1},{1,2},{2,3},{3,4},{4,5},{5,6},{6,7},{7,0},{8,9},{9,10},{10,1... | collective-permute-start | bytes 3145736 | tf_op jit(solution)/shard_map/ppermute | solution.py:26
  334.5 30.5 %copy-start.21 = (bf16[256,2048]{1,0:T(8,128)(2,1)S(1)}, bf16[256,2048]{1,0:T(8,128)(2,1)}, u32[]{:S(2)}) copy-start(bf16[256,2048]{1,0:T(8,128)(2,1)} %copy-done.20) | copy-start | bytes 3145732
  334.5 31.5 %copy-start.19 = (bf16[256,2048]{1,0:T(8,128)(2,1)S(1)}, bf16[256,2048]{1,0:T(8,128)(2,1)}, u32[]{:S(2)}) copy-start(bf16[256,2048]{1,0:T(8,128)(2,1)} %copy-done.18) | copy-start | bytes 3145732
  334.5 32.5 %copy-start.8 = (bf16[256,2048]{1,0:T(8,128)(2,1)S(1)}, bf16[256,2048]{1,0:T(8,128)(2,1)}, u32[]{:S(2)}) copy-start(bf16[256,2048]{1,0:T(8,128)(2,1)} %param.25) | copy-start | bytes 3145732
  334.5 38.1 %collective-permute-start.6 = (bf16[256,2048]{1,0:T(8,128)(2,1)}, bf16[256,2048]{1,0:T(8,128)(2,1)S(1)}, u32[]{:S(2)}, u32[]{:S(2)}) collective-permute-start(bf16[256,2048]{1,0:T(8,128)(2,1)} %collective-permute-done.5), channel_id=1, source_target_pairs={{1,0},{2,1},{3,2},{4,3},{5,4},{6,5},{7,6},{0,7},{9,8},{10,9},{11,1... | collective-permute-start | bytes 3145736 | tf_op jit(solution)/shard_map/ppermute | solution.py:28
  382.0 19.0 %copy-start.9 = (bf16[8,256,2048]{2,1,0:T(8,128)(2,1)S(1)}, bf16[8,256,2048]{2,1,0:T(8,128)(2,1)}, u32[]{:S(2)}) copy-start(bf16[8,256,2048]{2,1,0:T(8,128)(2,1)} %gather_fusion) | copy-start | bytes 25165828
  382.0 32.8 %slice-start.2 = ((s8[5767168]{0:T(1024)(128)(4,1)}), s8[4194304]{0:T(1024)(128)(4,1)S(1)}, s32[]{:S(2)}) async-start(s8[5767168]{0:T(1024)(128)(4,1)} %bitcast.302), calls=%async_computation.18 | async-start | bytes 8388608
  400.9 13.8 slice-start.3
  432.4 135.4 %all-gather.8.cloned.1.call-start = ((), (), s32[]{:S(2)}) async-start(), calls=%async_computation.11 | async-start | bytes 9437184 | tf_op jit(solution)/shard_map/all_gather | solution.py:224
  509.1 65.7 %copy-start.40 = (f32[256]{0:T(256)}, f32[256]{0:T(256)S(1)}, u32[]{:S(2)}) copy-start(f32[256]{0:T(256)S(1)} %get-tuple-element.329) | copy-start | bytes 3076
  509.1 65.7 %copy-start.42 = (f32[256]{0:T(256)}, f32[256]{0:T(256)S(1)}, u32[]{:S(2)}) copy-start(f32[256]{0:T(256)S(1)} %get-tuple-element.330) | copy-start | bytes 3076
  513.4 407.6 %reduce-scatter.17.cloned.1.call-start = ((), (), s32[]{:S(2)}) async-start(), calls=%async_computation.12 | async-start | bytes 9437184 | tf_op jit(solution)/shard_map/reduce_scatter | solution.py:279
  614.0 12.2 copy-start.2
  675.5 12.2 copy-start.2
  737.0 12.2 copy-start.2
  798.5 12.2 copy-start.2
  849.4 146.6 %reduce-scatter.13.cloned.1.call-start = ((), (), s32[]{:S(2)}) async-start(), calls=%async_computation.9 | async-start | bytes 9437184 | tf_op jit(solution)/shard_map/reduce_scatter | solution.py:195
  863.3 170.5 %reduce-scatter.19.cloned.1.call-start = ((), (), s32[]{:S(2)}) async-start(), calls=%async_computation.13 | async-start | bytes 589824
  863.3 14.1 copy-start.47
  863.3 14.1 copy-start.48
  877.4 17.7 %copy-start.39 = (bf16[2048]{0:T(1024)(128)(2,1)S(1)}, bf16[2048]{0:T(1024)(128)(2,1)}, u32[]{:S(2)}) copy-start(bf16[2048]{0:T(1024)(128)(2,1)} %get-tuple-element.234) | copy-start | bytes 12292
  895.1 27.3 %copy-start.29 = (f32[1,2048]{1,0:T(1,128)S(1)}, f32[1,2048]{1,0:T(1,128)}, u32[]{:S(2)}) copy-start(f32[1,2048]{1,0:T(1,128)} %copy-done.28) | copy-start | bytes 24580
  895.1 27.3 %copy-start.34 = (f32[256]{0:T(256)S(1)}, f32[256]{0:T(256)}, u32[]{:S(2)}) copy-start(f32[256]{0:T(256)} %copy-done.33) | copy-start | bytes 3076
  895.1 27.3 %copy-start.38 = (f32[256]{0:T(256)S(1)}, f32[256]{0:T(256)}, u32[]{:S(2)}) copy-start(f32[256]{0:T(256)} %copy-done.37) | copy-start | bytes 3076
  926.1 144.9 %reduce-scatter.21.cloned.1.call-start = ((), (), s32[]{:S(2)}) async-start(), calls=%async_computation.14 | async-start | bytes 589824
  927.2 581.8 %all-reduce.5.cloned.1.call-start = ((), (), s32[]{:S(2)}) async-start(), calls=%async_computation.15 | async-start | bytes 25690112 | tf_op jit(solution)/shard_map/psum | solution.py:304
  935.0 61.0 %copy-start.27 = (f32[1,2048]{1,0:T(1,128)S(1)}, f32[1,2048]{1,0:T(1,128)}, u32[]{:S(2)}) copy-start(f32[1,2048]{1,0:T(1,128)} %get-tuple-element.321) | copy-start | bytes 24580
  935.0 61.0 %copy-start.31 = (f32[256]{0:T(256)S(1)}, f32[256]{0:T(256)}, u32[]{:S(2)}) copy-start(f32[256]{0:T(256)} %copy-done.30) | copy-start | bytes 3076
  935.0 61.0 %copy-start.36 = (f32[256]{0:T(256)S(1)}, f32[256]{0:T(256)}, u32[]{:S(2)}) copy-start(f32[256]{0:T(256)} %copy-done.35) | copy-start | bytes 3076
  935.0 61.0 %copy-start.41 = (f32[256]{0:T(256)S(1)}, f32[256]{0:T(256)}, u32[]{:S(2)}) copy-start(f32[256]{0:T(256)} %copy-done.40) | copy-start | bytes 3076
  935.0 61.0 %copy-start.43 = (f32[256]{0:T(256)S(1)}, f32[256]{0:T(256)}, u32[]{:S(2)}) copy-start(f32[256]{0:T(256)} %copy-done.42) | copy-start | bytes 3076
  1509.0 10.0 slice-start
  (37 other events, 139.9 us)
Sparse Core Ops, SparseCore 0:
  16.2 56.9 all-gather.3
  161.7 71.4 reduce-scatter.10
  239.1 76.9 all-gather.5
  432.5 73.0 reduce-scatter.14
  513.5 54.2 all-gather.7
  849.5 71.4 reduce-scatter.16
  924.5 71.4 reduce-scatter.12
  999.6 34.1 reduce-scatter.18
  1036.9 34.0 reduce-scatter.20
  1074.3 434.6 all-reduce.4
